TPU v7x, 32 devices: a whole 2x2x4 slice. The times are simulated.
32 devices in a mesh: ga: 8 (over y, x, core), ba: 4 (over z).
Axes of the slice: x: 2, y: 2, z: 4, core: 2. Of those that a mesh axis runs over, the one named last changes fastest.
Arguments:
- psi: float32 [2, 16384, 2048], P(None, 'ga', 'ba'), may hold values from -0.1875 to 0.1875
- dpsi: float32 [2, 16384, 512], P(None, 'ga', 'ba'), may hold values from -6 to 6
- band_weight: float32 [2048], replicated, may hold values from 0.25 to 1
- panel_band: int32 [16], P('ba'), may hold values from 0 to 15, each once
- slab_offset: int32 [8], replicated, may hold values from 0 to 2047
Outputs:
- projected: float32 [2, 16384, 512], P(None, 'ga', 'ba')
Inputs may be any that keep to these rules, and one draw needn't show every extreme that they name: panel_band is a permutation of the panel numbers.
All inputs are finite; a program needn't handle non-finite values.
Results may differ from a plain program's by a relative error of at most 0.00012.
Values sent between devices are 32-bit elements; how exact they have to be, the bound alone decides.
A program may use at most 128 MiB of HBM per device.

v0:
```python
import jax
import jax.numpy as jnp
from jax import lax
from jax.sharding import PartitionSpec as P

PANEL = 128


def tdot(left, right):
    return lax.dot_general(
        left,
        right,
        (((0,), (0,)), ((), ())),
        precision=lax.Precision.HIGHEST,
        preferred_element_type=jnp.float32,
    )


def mdot(left, right):
    return jnp.dot(left, right, precision=lax.Precision.HIGHEST, preferred_element_type=jnp.float32)


def margin_of(waves, columns):
    over_re = tdot(waves[0], columns[0]) + tdot(waves[1], columns[1])
    over_im = tdot(waves[0], columns[1]) - tdot(waves[1], columns[0])
    return jnp.stack([over_re, over_im])


def correct_with(waves, weighted):
    corr_re = mdot(waves[0], weighted[0]) - mdot(waves[1], weighted[1])
    corr_im = mdot(waves[0], weighted[1]) + mdot(waves[1], weighted[0])
    return jnp.stack([corr_re, corr_im])


def weights_for(band_weight, panels):
    table = band_weight.reshape(-1, PANEL)
    onehot = (panels[:, None] == jnp.arange(table.shape[0], dtype=jnp.int32)[None, :]).astype(
        jnp.float32
    )
    return mdot(onehot, table).reshape(-1)


def per_device(psi, dpsi, band_weight, panel_band, slab_offset):
    offset = slab_offset[lax.axis_index("ga")]
    aligned = jnp.roll(dpsi, -offset, axis=1)
    local_weight = weights_for(band_weight, panel_band)
    blocks = margin_of(psi, lax.all_gather(aligned, "ba", axis=2, tiled=True))
    margin = lax.psum(blocks, "ga")
    weighted = margin * local_weight[None, :, None]
    correction = correct_with(psi, weighted)
    share = lax.psum_scatter(correction, "ba", scatter_dimension=2, tiled=True)
    result = aligned - share
    return jnp.roll(result, offset, axis=1)


def solution(mesh):
    in_specs = (P(None, "ga", "ba"), P(None, "ga", "ba"), P(), P("ba"), P())
    out_specs = P(None, "ga", "ba")
    return jax.shard_map(
        per_device, mesh=mesh, in_specs=in_specs, out_specs=out_specs, check_vma=False
    )
```

profile of v0, /device:TPU:0, one launch (start us, length us, event | category | flops | bytes accessed | tf_op | source)
XLA Modules:
  0.0 466.1 jit_solution(3996148815091841346)
XLA Ops:
  6.5 1.3 dynamic_slice.6
  9.1 1.9 copy.6
  11.0 2.5 fusion.29
  13.5 0.0 all-reduce.2.cloned.1.call-start
  13.6 152.4 %all-gather.2.cloned.1.call-done = f32[2,2048,512]{1,2,0:T(8,128)} async-done(((f32[2,2048,128]{1,2,0:T(8,128)}), f32[2,2048,512]{1,2,0:T(8,128)}) %all-gather.2.cloned.1.call-update) | async-done | bytes 8388624 | tf_op jit(solution)/shard_map/all_gather | solution.py:47
  166.0 9.4 %fusion.4 = f32[512,512]{1,0:T(8,128)S(1)} fusion(f32[2,2048,512]{1,2,0:T(8,128)} %all-gather.2.cloned.1.call-done, f32[2,2048,512]{2,1,0:T(8,128)} %param.7), kind=kOutput, calls=%fused_computation.11 | convolution fusion | flops 6442450944 | bytes 9437184 | tf_op jit(solution)/shard_map/dot_general | solution.py:10
  175.5 21.7 %fusion.6 = f32[512,512]{1,0:T(8,128)S(1)} fusion(f32[2,2048,512]{1,2,0:T(8,128)} %all-gather.2.cloned.1.call-done, f32[2,2048,512]{2,1,0:T(8,128)} %param.7), kind=kOutput, calls=%fused_computation.13 | convolution fusion | flops 6442450944 | bytes 9437184 | tf_op jit(solution)/shard_map/dot_general | solution.py:10
  197.3 6.8 %fusion.39 = f32[1,512,512]{1,2,0:T(8,128)S(1)} fusion(f32[512,512]{1,0:T(8,128)S(1)} %fusion.4, f32[2,2048,512]{2,1,0:T(8,128)S(1)} %bitcast.77, f32[2,2048,512]{1,2,0:T(8,128)S(1)} %bitcast.81), kind=kOutput, calls=%fused_computation.39 | convolution fusion | flops 6442713088 | bytes 10485760 | tf_op jit(solution)/shard_map/dot_general | solution.py:10
  204.1 6.8 %fusion.33 = f32[1,512,512]{1,2,0:T(8,128)S(1)} fusion(f32[512,512]{1,0:T(8,128)S(1)} %fusion.6, f32[2,2048,512]{2,1,0:T(8,128)S(1)} %bitcast.77, f32[2,2048,512]{1,2,0:T(8,128)S(1)} %bitcast.81), kind=kOutput, calls=%fused_computation.37 | convolution fusion | flops 6442713088 | bytes 10485760 | tf_op jit(solution)/shard_map/dot_general | solution.py:10
  211.0 1.5 pad_maximum_fusion.1
  212.5 0.0 all-reduce.2.cloned.1.call-update
  212.5 0.0 reduce-scatter.2.cloned.1.call-start
  212.6 0.2 convolution_bitcast_fusion
  212.7 59.8 %all-reduce.2.cloned.1.call-done = f32[2,512,512]{1,2,0:T(8,128)} async-done(((f32[2,512,512]{1,2,0:T(8,128)}), f32[2,512,512]{1,2,0:T(8,128)}) %all-reduce.2.cloned.1.call-update) | async-done | bytes 2097168 | tf_op jit(solution)/shard_map/psum | solution.py:48
  272.6 2.0 broadcast_multiply_fusion
  274.6 9.4 %fusion = f32[512,2048]{1,0:T(8,128)S(1)} fusion(f32[2,2048,512]{2,1,0:T(8,128)} %param.7, f32[2,512,512]{1,2,0:T(8,128)S(1)} %broadcast_multiply_fusion), kind=kOutput, calls=%fused_computation.7 | convolution fusion | flops 6442450944 | bytes 9437184 | tf_op jit(solution)/shard_map/dot_general | solution.py:20
  284.1 7.2 %fusion.2 = f32[512,2048]{1,0:T(8,128)S(1)} fusion(f32[2,2048,512]{2,1,0:T(8,128)S(1)} %bitcast.79, f32[2,512,512]{1,2,0:T(8,128)S(1)} %broadcast_multiply_fusion), kind=kOutput, calls=%fused_computation.9 | convolution fusion | flops 6442450944 | bytes 9437184 | tf_op jit(solution)/shard_map/dot_general | solution.py:20
  291.3 7.4 %add_bitcast_fusion = f32[1,2048,512]{1,2,0:T(8,128)S(1)} fusion(f32[512,2048]{1,0:T(8,128)S(1)} %fusion, f32[2,2048,512]{2,1,0:T(8,128)S(1)} %bitcast.79, f32[2,512,512]{1,2,0:T(8,128)S(1)} %broadcast_multiply_fusion), kind=kOutput, calls=%fused_computation.23 | convolution fusion | flops 6443499520 | bytes 13631488 | tf_op jit(solution)/shard_map/dot_general | solution.py:20
  298.7 7.2 %subtract_bitcast_fusion = f32[1,2048,512]{1,2,0:T(8,128)S(1)} fusion(f32[512,2048]{1,0:T(8,128)S(1)} %fusion.2, f32[2,2048,512]{2,1,0:T(8,128)S(1)} %bitcast.79, f32[2,512,512]{1,2,0:T(8,128)S(1)} %broadcast_multiply_fusion), kind=kOutput, calls=%fused_computation.24 | convolution fusion | flops 6443499520 | bytes 13631488 | tf_op jit(solution)/shard_map/dot_general | solution.py:20
  306.0 3.8 pad_maximum_fusion
  311.1 142.6 %reduce-scatter.2.cloned.1.call-done = f32[2,2048,128]{1,2,0:T(8,128)} async-done(((f32[2,2048,512]{1,2,0:T(8,128)}), f32[2,2048,128]{1,2,0:T(8,128)}) %reduce-scatter.2.cloned.1.call-update) | async-done | bytes 2097168 | tf_op jit(solution)/shard_map/reduce_scatter | solution.py:51
  453.7 2.8 fusion.44
  456.4 1.2 fusion.28
  457.6 1.8 copy.8
  (24 shorter events, 0.1 us)
Async XLA Ops:
  6.5 206.0 %copy-start = (f32[2048]{0:T(1024)S(1)}, f32[2048]{0:T(1024)}, u32[]{:S(2)}) copy-start(f32[2048]{0:T(1024)} %param.9) | copy-start | bytes 24580
  6.5 159.5 %all-gather.2.cloned.1.call-start = ((), (), s32[]{:S(2)}) async-start(), calls=%async_computation.1 | async-start | bytes 10485760 | tf_op jit(solution)/shard_map/all_gather | solution.py:47
  13.5 259.0 %all-reduce.2.cloned.1.call-start = ((), (), s32[]{:S(2)}) async-start(), calls=%async_computation.2 | async-start | bytes 4194304 | tf_op jit(solution)/shard_map/psum | solution.py:48
  166.0 31.2 %slice-start = ((s8[8388608]{0:T(1024)(128)(4,1)}), s8[4194304]{0:T(1024)(128)(4,1)S(1)}, s32[]{:S(2)}) async-start(s8[8388608]{0:T(1024)(128)(4,1)} %bitcast.76), calls=%async_computation.4 | async-start | bytes 8388608
  166.0 31.2 %slice-start.4 = ((s8[8388608]{0:T(1024)(128)(4,1)}), s8[4194304]{0:T(1024)(128)(4,1)S(1)}, s32[]{:S(2)}) async-start(s8[8388608]{0:T(1024)(128)(4,1)} %bitcast.80), calls=%async_computation.8 | async-start | bytes 8388608
  175.5 21.7 %slice-start.1 = ((s8[8388608]{0:T(1024)(128)(4,1)}), s8[4194304]{0:T(1024)(128)(4,1)S(1)}, s32[]{:S(2)}) async-start(s8[8388608]{0:T(1024)(128)(4,1)} %bitcast.76), calls=%async_computation.5 | async-start | bytes 8388608
  175.5 21.7 %slice-start.5 = ((s8[8388608]{0:T(1024)(128)(4,1)}), s8[4194304]{0:T(1024)(128)(4,1)S(1)}, s32[]{:S(2)}) async-start(s8[8388608]{0:T(1024)(128)(4,1)} %bitcast.80), calls=%async_computation.9 | async-start | bytes 8388608
  211.0 1.6 copy-start.2
  212.5 241.2 %reduce-scatter.2.cloned.1.call-start = ((), (), s32[]{:S(2)}) async-start(), calls=%async_computation.3 | async-start | bytes 10485760 | tf_op jit(solution)/shard_map/reduce_scatter | solution.py:51
  272.6 11.5 %slice-start.2 = ((s8[8388608]{0:T(1024)(128)(4,1)}), s8[4194304]{0:T(1024)(128)(4,1)S(1)}, s32[]{:S(2)}) async-start(s8[8388608]{0:T(1024)(128)(4,1)} %bitcast.78), calls=%async_computation.6 | async-start | bytes 8388608
  274.6 9.5 %slice-start.3 = ((s8[8388608]{0:T(1024)(128)(4,1)}), s8[4194304]{0:T(1024)(128)(4,1)S(1)}, s32[]{:S(2)}) async-start(s8[8388608]{0:T(1024)(128)(4,1)} %bitcast.78), calls=%async_computation.7 | async-start | bytes 8388608
  453.7 5.8 %copy-start.1 = (f32[2048]{0:T(1024)S(1)}, f32[2048]{0:T(1024)}, u32[]{:S(2)}) copy-start(f32[2048]{0:T(1024)} %param.9) | copy-start | bytes 24580
Sparse Core Ops, SparseCore 0:
  13.7 152.3 all-gather.1
  212.6 59.9 all-reduce.1
  309.9 143.6 reduce-scatter.1
where the time goes:
time: 472 us; the launch traced here: 466 us
  waiting for transfers between devices  355 us (75%)
  matrix products  76.3 us (16%)
  between operations  16 us (3%)
  other arithmetic  13.7 us (3%)
  local copies, waits for them, and re-layouts  5.08 us (1%)
    all_gather x1, waiting for transfers between devices, per_device(): blocks = margin_of(psi, lax.all_gather(aligned, 'ba', axis=2, tiled=True))  152 us
    reduce_scatter x1, waiting for transfers between devices, per_device(): share = lax.psum_scatter(correction, 'ba', scatter_dimension=2, tiled=True)  143 us
    psum x1, waiting for transfers between devices, per_device(): margin = lax.psum(blocks, 'ga')  59.8 us
    dot_general x4, matrix products, tdot(): lax.dot_general(left, right, (((0,), (0,)), ((), ())), precision=lax.Prec...  44.8 us
    dot_general x5, matrix products, mdot(): jnp.dot(left, right, precision=lax.Precision.HIGHEST, preferred_element_t...  31.5 us
  transfers between devices with their start and end apart: 3, of which 3 were waited for; matrix products, arithmetic and copies ran while one was open for 0% of the time, Pallas kernels for 0%

commit v1 on v0

v1 whole, which is shorter than its diff:
```python
import functools

import jax
import jax.numpy as jnp
from jax import lax
from jax.sharding import PartitionSpec as P

PANEL = 128


def tdot(left, right):
    return lax.dot_general(
        left,
        right,
        (((0,), (0,)), ((), ())),
        precision=lax.Precision.HIGH,
        preferred_element_type=jnp.float32,
    )


def mdot(left, right):
    return jnp.dot(left, right, precision=lax.Precision.HIGH, preferred_element_type=jnp.float32)


CHUNKS = 2


def turned(packed, width):
    column = lax.broadcasted_iota(jnp.int32, packed.shape, 1)
    first = (column // width) % 2 == 0
    return jnp.where(first, jnp.roll(packed, -width, axis=1), -jnp.roll(packed, width, axis=1))


def sum_over(block, axis, size):
    if size & (size - 1) or block.shape[0] % size:
        return lax.psum(block, axis)
    place = lax.axis_index(axis)
    bits = [1 << b for b in range(size.bit_length() - 1)]
    for bit in bits:
        upper = (place // bit) % 2
        half = block.shape[0] // 2
        kept = lax.dynamic_slice_in_dim(block, upper * half, half, 0)
        sent = lax.dynamic_slice_in_dim(block, (1 - upper) * half, half, 0)
        block = kept + lax.ppermute(sent, axis, [(i, i ^ bit) for i in range(size)])
    for bit in reversed(bits):
        upper = (place // bit) % 2 == 1
        other = lax.ppermute(block, axis, [(i, i ^ bit) for i in range(size)])
        block = jnp.concatenate([jnp.where(upper, other, block), jnp.where(upper, block, other)])
    return block


def weights_for(band_weight, panels):
    table = band_weight.reshape(-1, PANEL)
    onehot = (panels[:, None] == jnp.arange(table.shape[0], dtype=jnp.int32)[None, :]).astype(
        jnp.float32
    )
    return mdot(onehot, table).reshape(-1)


def per_device(size, psi, dpsi, band_weight, panel_band, slab_offset):
    offset = slab_offset[lax.axis_index("ga")]
    aligned = jnp.roll(dpsi, -offset, axis=1)
    local_weight = weights_for(band_weight, panel_band)
    width = aligned.shape[2] // CHUNKS
    pieces = []
    for chunk in range(CHUNKS):
        columns = slice(chunk * width, (chunk + 1) * width)
        own = jnp.concatenate([aligned[0, :, columns], aligned[1, :, columns]], axis=1)
        every = lax.all_gather(own, "ba", axis=1, tiled=True)
        block = tdot(psi[0], every) + turned(tdot(psi[1], every), width)
        weighted = sum_over(block, "ga", size) * local_weight[:, None]
        correction = mdot(psi[0], weighted) - mdot(psi[1], turned(weighted, width))
        share = lax.psum_scatter(correction, "ba", scatter_dimension=1, tiled=True)
        pieces.append(own - share)
    result = jnp.stack(
        [
            jnp.concatenate([piece[:, part * width : (part + 1) * width] for piece in pieces], axis=1)
            for part in range(2)
        ]
    )
    return jnp.roll(result, offset, axis=1)


def solution(mesh):
    in_specs = (P(None, "ga", "ba"), P(None, "ga", "ba"), P(), P("ba"), P())
    out_specs = P(None, "ga", "ba")
    return jax.shard_map(
        functools.partial(per_device, mesh.shape["ga"]), mesh=mesh, in_specs=in_specs, out_specs=out_specs, check_vma=False
    )
```

time: 472 us -> 426 us (0.903); the launches traced: 466 us -> 425 us
  waiting for transfers between devices: 355 us -> 311 us
  matrix products: 76.3 us -> 61.5 us
  starting transfers between devices: 0.09 us -> 11.2 us
  local copies, waits for them, and re-layouts: 5.08 us -> 12.8 us
    psum x1 -> x0, waiting for transfers between devices: 59.8 us -> none  [per_device(): margin = lax.psum(blocks, 'ga')]
    ppermute x0 -> x12, waiting for transfers between devices: none -> 21.6 us  [the longest x6 12.9 us: sum_over(): block = kept + lax.ppermute(sent, axis, [(i, i ^ bit) for i in range(size)])]
    dot_general x4, matrix products: 44.8 us -> 24.3 us  [tdot(): lax.dot_general(left, right, (((0,), (0,)), ((), ())), precision=lax.Prec...]
    ppermute x0 -> x12, starting transfers between devices: none -> 11 us  [the longest x6 5.82 us: sum_over(): block = kept + lax.ppermute(sent, axis, [(i, i ^ bit) for i in range(size)])]
    reduce_scatter x1 -> x2, waiting for transfers between devices: 143 us -> 135 us  [per_device(): share = lax.psum_scatter(correction, 'ba', scatter_dimension=1, tiled=True)]
    dot_general x5, matrix products: 31.5 us -> 37.1 us  [mdot(): jnp.dot(left, right, precision=lax.Precision.HIGH, preferred_element_type...]
    another operation x2, other arithmetic: 5.31 us -> 0.18 us  [per_device(): jnp.stack([jnp.concatenate([piece[:, part * width:(part + 1) * width] for...]
    all_gather x1 -> x2, waiting for transfers between devices: 152 us -> 154 us  [per_device(): every = lax.all_gather(own, 'ba', axis=1, tiled=True)]
  transfers between devices with their start and end apart: 3 -> 16, of which waited for: 3 -> 12; matrix products, arithmetic and copies ran while one was open for 0% -> 10% of each run, Pallas kernels for 0% -> 0%
where the time goes in v1:
time: 426 us; the launch traced here: 425 us
  waiting for transfers between devices  311 us (73%)
  matrix products  61.5 us (14%)
  between operations  15.9 us (4%)
  other arithmetic  13.5 us (3%)
  local copies, waits for them, and re-layouts  12.8 us (3%)
  starting transfers between devices  11.2 us (3%)
    all_gather x2, waiting for transfers between devices, per_device(): every = lax.all_gather(own, 'ba', axis=1, tiled=True)  154 us
    reduce_scatter x2, waiting for transfers between devices, per_device(): share = lax.psum_scatter(correction, 'ba', scatter_dimension=1, tiled=True)  135 us
    dot_general x5, matrix products, mdot(): jnp.dot(left, right, precision=lax.Precision.HIGH, preferred_element_type...  37.1 us
    dot_general x4, matrix products, tdot(): lax.dot_general(left, right, (((0,), (0,)), ((), ())), precision=lax.Prec...  24.3 us
    ppermute x6, waiting for transfers between devices, sum_over(): block = kept + lax.ppermute(sent, axis, [(i, i ^ bit) for i in range(size)])  12.9 us
    ppermute x6, waiting for transfers between devices, sum_over(): other = lax.ppermute(block, axis, [(i, i ^ bit) for i in range(size)])  8.7 us
  transfers between devices with their start and end apart: 16, of which 12 were waited for; matrix products, arithmetic and copies ran while one was open for 10% of the time, Pallas kernels for 0%

profile of v1, /device:TPU:0, one launch (start us, length us, event | category | flops | bytes accessed | tf_op | source)
XLA Modules:
  0.0 425.5 jit_solution(11217355059980172161)
XLA Ops:
  8.9 1.9 copy.6
  14.5 82.4 %all-gather.5.cloned.1.call-done = f32[2048,512]{0,1:T(8,128)} async-done(((f32[2048,128]{0,1:T(8,128)}), f32[2048,512]{0,1:T(8,128)}) %all-gather.5.cloned.1.call-update) | async-done | bytes 4194320 | tf_op jit(solution)/shard_map/all_gather | solution.py:69
  96.9 6.5 %fusion.41 = f32[512,512]{1,0:T(8,128)S(1)} fusion(f32[2048,512]{0,1:T(8,128)} %all-gather.5.cloned.1.call-done, f32[2,2048,512]{2,1,0:T(8,128)} %param.7), kind=kOutput, calls=%fused_computation.44 | convolution fusion | flops 3221225472 | bytes 9437184 | tf_op jit(solution)/shard_map/dot_general | solution.py:12
  104.2 1.7 fusion.80
  105.9 71.8 %all-gather.3.cloned.1.call-done = f32[2048,512]{0,1:T(8,128)} async-done(((f32[2048,128]{0,1:T(8,128)}), f32[2048,512]{0,1:T(8,128)}) %all-gather.3.cloned.1.call-update) | async-done | bytes 4194320 | tf_op jit(solution)/shard_map/all_gather | solution.py:69
  177.8 6.7 %fusion.38 = f32[512,512]{1,0:T(8,128)S(1)} fusion(f32[2048,512]{0,1:T(8,128)} %all-gather.3.cloned.1.call-done, f32[2,2048,512]{2,1,0:T(8,128)} %param.7), kind=kOutput, calls=%fused_computation.43 | convolution fusion | flops 3221225472 | bytes 9437184 | tf_op jit(solution)/shard_map/dot_general | solution.py:12
  185.7 6.3 %fusion.44 = f32[512,512]{1,0:T(8,128)S(1)} fusion(f32[2048,512]{0,1:T(8,128)S(1)} %copy-done.3, f32[2,2048,512]{2,1,0:T(8,128)} %param.7, f32[512,64]{1,0:T(8,128)S(1)} %copy-done.6, f32[512,448]{1,0:T(8,128)S(1)} %copy-done.5, f32[512,448]{1,0:T(8,128)S(1)} %copy-done.4, f32[512,64]{1,0:T(8,128)S(1)} %get-tuple-element.30, ...), kind=kOutput, calls=%fused_computation.45 | convolution fusion | flops 3225944064 | bytes 11538944 | tf_op jit(solution)/shard_map/dot_general | solution.py:12
  192.8 4.9 %fusion.47 = f32[512,512]{1,0:T(8,128)} fusion(f32[2048,512]{0,1:T(8,128)S(1)} %copy-done.2, f32[2,2048,512]{2,1,0:T(8,128)S(1)} %bitcast.75, f32[512,64]{1,0:T(8,128)S(1)} %get-tuple-element.21, f32[512,448]{1,0:T(8,128)S(1)} %get-tuple-element.23, f32[512,448]{1,0:T(8,128)S(1)} %get-tuple-element.22, f32[512,64]{1,0:T(8,128)S(1)} %get-tuple-element.20, ...), kind=kOutput, calls=%fused_computation.46 | convolution fusion | flops 3225944064 | bytes 12063232 | tf_op jit(solution)/shard_map/dot_general | solution.py:12
  197.7 1.9 constant_dynamic-slice_fusion.5
  204.8 5.7 %collective-permute-done.7 = f32[128,512]{1,0:T(8,128)S(1)} collective-permute-done((f32[128,512]{1,0:T(8,128)S(1)}, f32[128,512]{1,0:T(8,128)S(1)}, u32[]{:S(2)}, u32[]{:S(2)}) %collective-permute-start.7) | collective-permute-done | bytes 262176 | tf_op jit(solution)/shard_map/ppermute | solution.py:44
  212.1 3.0 collective-permute-done.1
  215.2 1.6 collective-permute-start.2
  217.4 4.2 collective-permute-done.2
  221.6 1.6 collective-permute-start.3
  228.2 4.0 collective-permute-done.10
  233.1 1.9 collective-permute-done.4
  240.1 9.8 %fusion.4 = f32[512,2048]{1,0:T(8,128)S(1)} fusion(f32[2,2048,512]{2,1,0:T(8,128)} %param.7, f32[512,64]{1,0:T(8,128)S(1)} %get-tuple-element.15, f32[512,448]{1,0:T(8,128)S(1)} %get-tuple-element.17, f32[512,448]{1,0:T(8,128)S(1)} %get-tuple-element.16, f32[512,64]{1,0:T(8,128)S(1)} %get-tuple-element.14, s32[512]{0:T(512)S(1)} %iota_shift-right-logical_fusion, ...), kind=kOutput, calls=%fused_computation.10 | convolution fusion | flops 3225681920 | bytes 10490368 | tf_op jit(solution)/shard_map/dot_general | solution.py:22
  249.9 8.8 %subtract_bitcast_fusion.1 = f32[2048,512]{0,1:T(8,128)} fusion(f32[512,2048]{1,0:T(8,128)S(1)} %fusion.4, f32[512,512]{1,0:T(8,128)S(1)} %get-tuple-element.42, f32[2,2048,512]{2,1,0:T(8,128)S(1)} %bitcast.77), kind=kOutput, calls=%fused_computation.23 | convolution fusion | flops 3222274048 | bytes 13631488 | tf_op jit(solution)/shard_map/dot_general | solution.py:22
  259.4 9.8 %fusion = f32[512,2048]{1,0:T(8,128)S(1)} fusion(f32[2,2048,512]{2,1,0:T(8,128)} %param.7, f32[512,64]{1,0:T(8,128)S(1)} %get-tuple-element.25, f32[512,448]{1,0:T(8,128)S(1)} %get-tuple-element.27, f32[512,448]{1,0:T(8,128)S(1)} %get-tuple-element.26, f32[512,64]{1,0:T(8,128)S(1)} %get-tuple-element.24, s32[512]{0:T(512)S(1)} %iota_shift-right-logical_fusion, ...), kind=kOutput, calls=%fused_computation.6 | convolution fusion | flops 3225681920 | bytes 10490368 | tf_op jit(solution)/shard_map/dot_general | solution.py:22
  269.2 8.6 %subtract_bitcast_fusion = f32[2048,512]{0,1:T(8,128)} fusion(f32[512,2048]{1,0:T(8,128)S(1)} %fusion, f32[512,512]{1,0:T(8,128)S(1)} %get-tuple-element.43, f32[2,2048,512]{2,1,0:T(8,128)S(1)} %bitcast.79), kind=kOutput, calls=%fused_computation.22 | convolution fusion | flops 3222274048 | bytes 13631488 | tf_op jit(solution)/shard_map/dot_general | solution.py:22
  278.9 55.3 %reduce-scatter.3.cloned.1.call-done = f32[2048,128]{0,1:T(8,128)} async-done(((f32[2048,512]{0,1:T(8,128)}), f32[2048,128]{0,1:T(8,128)}) %reduce-scatter.3.cloned.1.call-update) | async-done | bytes 1048592 | tf_op jit(solution)/shard_map/reduce_scatter | solution.py:73
  334.2 79.5 %reduce-scatter.5.cloned.1.call-done = f32[2048,128]{0,1:T(8,128)} async-done(((f32[2048,512]{0,1:T(8,128)}), f32[2048,128]{0,1:T(8,128)}) %reduce-scatter.5.cloned.1.call-update) | async-done | bytes 1048592 | tf_op jit(solution)/shard_map/reduce_scatter | solution.py:73
  413.7 2.0 fusion.67
  417.1 1.8 copy.10
  (99 shorter events, 28.1 us)
Async XLA Ops:
  6.5 229.3 %copy-start = (f32[2048]{0:T(1024)S(1)}, f32[2048]{0:T(1024)}, u32[]{:S(2)}) copy-start(f32[2048]{0:T(1024)} %param.9) | copy-start | bytes 24580
  6.5 90.4 %all-gather.5.cloned.1.call-start = ((), (), s32[]{:S(2)}) async-start(), calls=%async_computation.4 | async-start | bytes 5242880 | tf_op jit(solution)/shard_map/all_gather | solution.py:69
  13.3 164.4 %all-gather.3.cloned.1.call-start = ((), (), s32[]{:S(2)}) async-start(), calls=%async_computation.2 | async-start | bytes 5242880 | tf_op jit(solution)/shard_map/all_gather | solution.py:69
  14.4 319.8 %reduce-scatter.3.cloned.1.call-start = ((), (), s32[]{:S(2)}) async-start(), calls=%async_computation.3 | async-start | bytes 5242880 | tf_op jit(solution)/shard_map/reduce_scatter | solution.py:73
  177.8 7.2 %copy-start.6 = (f32[512,64]{1,0:T(8,128)S(1)}, f32[512,64]{1,0:T(8,128)}, u32[]{:S(2)}) copy-start(f32[512,64]{1,0:T(8,128)} %get-tuple-element.31) | copy-start | bytes 393220
  184.4 8.4 %slice-start = ((s8[8388608]{0:T(1024)(128)(4,1)}), s8[4194304]{0:T(1024)(128)(4,1)S(1)}, s32[]{:S(2)}) async-start(s8[8388608]{0:T(1024)(128)(4,1)} %bitcast.74), calls=%async_computation.6 | async-start | bytes 8388608
  192.8 7.3 %collective-permute-start.6 = (f32[256,512]{1,0:T(8,128)}, f32[256,512]{1,0:T(8,128)}, u32[]{:S(2)}, u32[]{:S(2)}) collective-permute-start(f32[256,512]{1,0:T(8,128)} %constant_dynamic-slice_fusion.2), channel_id=1, source_target_pairs={{0,4},{4,0},{8,12},{12,8},{16,20},{20,16},{24,28},{28,24},{1,5},{5... | collective-permute-start | bytes 1572872 | tf_op jit(solution)/shard_map/ppermute | solution.py:44
  199.6 3.2 collective-permute-start
  201.2 9.2 %collective-permute-start.7 = (f32[128,512]{1,0:T(8,128)S(1)}, f32[128,512]{1,0:T(8,128)S(1)}, u32[]{:S(2)}, u32[]{:S(2)}) collective-permute-start(f32[128,512]{1,0:T(8,128)S(1)} %constant_dynamic-slice_fusion.1), channel_id=1, source_target_pairs={{0,8},{4,12},{8,0},{12,4},{16,24},{20,28},{24,16},{28,20},{1,9},{5... | collective-permute-start | bytes 786440 | tf_op jit(solution)/shard_map/ppermute | solution.py:44
  204.1 11.1 %collective-permute-start.1 = (f32[128,512]{1,0:T(8,128)S(1)}, f32[128,512]{1,0:T(8,128)S(1)}, u32[]{:S(2)}, u32[]{:S(2)}) collective-permute-start(f32[128,512]{1,0:T(8,128)S(1)} %constant_dynamic-slice_fusion.4), channel_id=1, source_target_pairs={{0,8},{4,12},{8,0},{12,4},{16,24},{20,28},{24,16},{28,20},{1,9},{5... | collective-permute-start | bytes 786440 | tf_op jit(solution)/shard_map/ppermute | solution.py:44
  210.5 25.4 %copy-start.7 = (s32[4]{0:T(128)S(1)}, s32[4]{0:T(128)}, u32[]{:S(2)}) copy-start(s32[4]{0:T(128)} %param.10) | copy-start | bytes 52
  210.6 6.2 %collective-permute-start.8 = (f32[64,512]{1,0:T(8,128)S(1)}, f32[64,512]{1,0:T(8,128)S(1)}, u32[]{:S(2)}, u32[]{:S(2)}) collective-permute-start(f32[64,512]{1,0:T(8,128)S(1)} %constant_dynamic-slice_fusion), channel_id=1, source_target_pairs={{0,16},{4,20},{8,24},{12,28},{16,0},{20,4},{24,8},{28,12},{1,17},{... | collective-permute-start | bytes 393224 | tf_op jit(solution)/shard_map/ppermute | solution.py:44
  215.2 6.3 %collective-permute-start.2 = (f32[64,512]{1,0:T(8,128)S(1)}, f32[64,512]{1,0:T(8,128)S(1)}, u32[]{:S(2)}, u32[]{:S(2)}) collective-permute-start(f32[64,512]{1,0:T(8,128)S(1)} %constant_dynamic-slice_fusion.3), channel_id=1, source_target_pairs={{0,16},{4,20},{8,24},{12,28},{16,0},{20,4},{24,8},{28,12},{1,17},{... | collective-permute-start | bytes 393224 | tf_op jit(solution)/shard_map/ppermute | solution.py:44
  216.8 7.3 %collective-permute-start.9 = (f32[64,512]{1,0:T(8,128)S(1)}, f32[64,512]{1,0:T(8,128)S(1)}, u32[]{:S(2)}, u32[]{:S(2)}) collective-permute-start(f32[64,512]{1,0:T(8,128)S(1)} %dynamic-slice_add_fusion.4), channel_id=1, source_target_pairs={{0,16},{4,20},{8,24},{12,28},{16,0},{20,4},{24,8},{28,12},{1,17},{... | collective-permute-start | bytes 393224 | tf_op jit(solution)/shard_map/ppermute | solution.py:47
  221.6 5.0 %collective-permute-start.3 = (f32[64,512]{1,0:T(8,128)S(1)}, f32[64,512]{1,0:T(8,128)S(1)}, u32[]{:S(2)}, u32[]{:S(2)}) collective-permute-start(f32[64,512]{1,0:T(8,128)S(1)} %dynamic-slice_add_fusion.5), channel_id=1, source_target_pairs={{0,16},{4,20},{8,24},{12,28},{16,0},{20,4},{24,8},{28,12},{1,17},{... | collective-permute-start | bytes 393224 | tf_op jit(solution)/shard_map/ppermute | solution.py:47
  224.1 8.1 %collective-permute-start.10 = (f32[128,512]{1,0:T(8,128)S(1)}, f32[128,512]{1,0:T(8,128)S(1)}, u32[]{:S(2)}, u32[]{:S(2)}) collective-permute-start(f32[128,512]{1,0:T(8,128)S(1)} %pad_maximum_fusion.5), channel_id=1, source_target_pairs={{0,8},{4,12},{8,0},{12,4},{16,24},{20,28},{24,16},{28,20},{1,9},{5... | collective-permute-start | bytes 786440 | tf_op jit(solution)/shard_map/ppermute | solution.py:47
  226.7 8.3 %collective-permute-start.4 = (f32[128,512]{1,0:T(8,128)S(1)}, f32[128,512]{1,0:T(8,128)S(1)}, u32[]{:S(2)}, u32[]{:S(2)}) collective-permute-start(f32[128,512]{1,0:T(8,128)S(1)} %pad_maximum_fusion.4), channel_id=1, source_target_pairs={{0,8},{4,12},{8,0},{12,4},{16,24},{20,28},{24,16},{28,20},{1,9},{5... | collective-permute-start | bytes 786440 | tf_op jit(solution)/shard_map/ppermute | solution.py:47
  233.1 3.0 collective-permute-start.11
  235.9 2.3 collective-permute-start.5
  239.5 10.4 %slice-start.2 = ((s8[8388608]{0:T(1024)(128)(4,1)}), s8[4194304]{0:T(1024)(128)(4,1)S(1)}, s32[]{:S(2)}) async-start(s8[8388608]{0:T(1024)(128)(4,1)} %bitcast.76), calls=%async_computation.8 | async-start | bytes 8388608
  240.1 9.9 %slice-start.3 = ((s8[8388608]{0:T(1024)(128)(4,1)}), s8[4194304]{0:T(1024)(128)(4,1)S(1)}, s32[]{:S(2)}) async-start(s8[8388608]{0:T(1024)(128)(4,1)} %bitcast.76), calls=%async_computation.9 | async-start | bytes 8388608
  258.8 154.9 %reduce-scatter.5.cloned.1.call-start = ((), (), s32[]{:S(2)}) async-start(), calls=%async_computation.5 | async-start | bytes 5242880 | tf_op jit(solution)/shard_map/reduce_scatter | solution.py:73
  259.0 10.2 %slice-start.4 = ((s8[8388608]{0:T(1024)(128)(4,1)}), s8[4194304]{0:T(1024)(128)(4,1)S(1)}, s32[]{:S(2)}) async-start(s8[8388608]{0:T(1024)(128)(4,1)} %bitcast.78), calls=%async_computation.10 | async-start | bytes 8388608
  259.4 9.8 %slice-start.5 = ((s8[8388608]{0:T(1024)(128)(4,1)}), s8[4194304]{0:T(1024)(128)(4,1)S(1)}, s32[]{:S(2)}) async-start(s8[8388608]{0:T(1024)(128)(4,1)} %bitcast.78), calls=%async_computation.11 | async-start | bytes 8388608
  (6 other events, 33.1 us)
Sparse Core Ops, SparseCore 0:
  13.4 83.4 all-gather.4
  98.5 79.2 all-gather.2
  258.9 75.2 reduce-scatter.2
  336.3 77.2 reduce-scatter.4

commit v2 on v1

--- a/solution.py
+++ b/solution.py
@@ -62,16 +62,21 @@
     aligned = jnp.roll(dpsi, -offset, axis=1)
     local_weight = weights_for(band_weight, panel_band)
     width = aligned.shape[2] // CHUNKS
-    pieces = []
+    owns, corrections = [], []
     for chunk in range(CHUNKS):
         columns = slice(chunk * width, (chunk + 1) * width)
         own = jnp.concatenate([aligned[0, :, columns], aligned[1, :, columns]], axis=1)
         every = lax.all_gather(own, "ba", axis=1, tiled=True)
+        if corrections:
+            every, corrections[-1] = lax.optimization_barrier((every, corrections[-1]))
         block = tdot(psi[0], every) + turned(tdot(psi[1], every), width)
         weighted = sum_over(block, "ga", size) * local_weight[:, None]
-        correction = mdot(psi[0], weighted) - mdot(psi[1], turned(weighted, width))
-        share = lax.psum_scatter(correction, "ba", scatter_dimension=1, tiled=True)
-        pieces.append(own - share)
+        owns.append(own)
+        corrections.append(mdot(psi[0], weighted) - mdot(psi[1], turned(weighted, width)))
+    pieces = [
+        own - lax.psum_scatter(correction, "ba", scatter_dimension=1, tiled=True)
+        for own, correction in zip(owns, corrections)
+    ]
     result = jnp.stack(
         [
             jnp.concatenate([piece[:, part * width : (part + 1) * width] for piece in pieces], axis=1)

time: 426 us -> 347 us (0.81)
  waiting for transfers between devices: 311 us -> 234 us
    all_gather x2, waiting for transfers between devices: 154 us -> 94.5 us  [per_device(): every = lax.all_gather(own, 'ba', axis=1, tiled=True)]
    reduce_scatter x2, waiting for transfers between devices: 135 us -> 94.6 us  [per_device(): lax.psum_scatter(correction, 'ba', scatter_dimension=1, tiled=True)]
    ppermute x6, waiting for transfers between devices: 12.9 us -> 24.4 us  [sum_over(): block = kept + lax.ppermute(sent, axis, [(i, i ^ bit) for i in range(size)])]
    ppermute x6, waiting for transfers between devices: 8.7 us -> 20.2 us  [sum_over(): other = lax.ppermute(block, axis, [(i, i ^ bit) for i in range(size)])]
  transfers between devices with their start and end apart: 16 -> 16, of which waited for: 12 -> 16; matrix products, arithmetic and copies ran while one was open for 10% -> 20% of each run, Pallas kernels for 0% -> 0%
where the time goes in v2:
time: 347 us
  waiting for transfers between devices  234 us (67%)
  matrix products  59.9 us (17%)
  between operations  15.9 us (5%)
  starting transfers between devices  13.5 us (4%)
  local copies, waits for them, and re-layouts  13.3 us (4%)
  other arithmetic  10.4 us (3%)
    reduce_scatter x2, waiting for transfers between devices, per_device(): lax.psum_scatter(correction, 'ba', scatter_dimension=1, tiled=True)  94.6 us
    all_gather x2, waiting for transfers between devices, per_device(): every = lax.all_gather(own, 'ba', axis=1, tiled=True)  94.5 us
    dot_general x5, matrix products, mdot(): jnp.dot(left, right, precision=lax.Precision.HIGH, preferred_element_type...  34.9 us
    dot_general x4, matrix products, tdot(): lax.dot_general(left, right, (((0,), (0,)), ((), ())), precision=lax.Prec...  25 us
    ppermute x6, waiting for transfers between devices, sum_over(): block = kept + lax.ppermute(sent, axis, [(i, i ^ bit) for i in range(size)])  24.4 us
    ppermute x6, waiting for transfers between devices, sum_over(): other = lax.ppermute(block, axis, [(i, i ^ bit) for i in range(size)])  20.2 us
  transfers between devices with their start and end apart: 16, of which 16 were waited for; matrix products, arithmetic and copies ran while one was open for 20% of the time, Pallas kernels for 0%

profile of v2, /device:TPU:0, one launch (start us, length us, event | category | flops | bytes accessed | tf_op | source)
XLA Modules:
  0.0 346.7 jit_solution(5663664512739268655)
XLA Ops:
  14.5 82.4 %all-gather.5.cloned.1.call-done = f32[2048,512]{0,1:T(8,128)} async-done(((f32[2048,128]{0,1:T(8,128)}), f32[2048,512]{0,1:T(8,128)}) %all-gather.5.cloned.1.call-update) | async-done | bytes 4194320 | tf_op jit(solution)/shard_map/all_gather | solution.py:69
  96.9 6.5 %fusion.38 = f32[512,512]{1,0:T(8,128)S(1)} fusion(f32[2048,512]{0,1:T(8,128)} %all-gather.5.cloned.1.call-done, f32[2,2048,512]{2,1,0:T(8,128)} %param.7), kind=kOutput, calls=%fused_computation.43 | convolution fusion | flops 3221225472 | bytes 9437184 | tf_op jit(solution)/shard_map/dot_general | solution.py:12
  104.0 2.1 copy-done.3
  106.1 6.0 %fusion.47 = f32[512,512]{1,0:T(8,128)S(1)} fusion(f32[2048,512]{0,1:T(8,128)S(1)} %copy-done.3, f32[2,2048,512]{2,1,0:T(8,128)} %param.7, f32[512,64]{1,0:T(8,128)S(1)} %get-tuple-element.35, f32[512,448]{1,0:T(8,128)S(1)} %get-tuple-element.37, f32[512,448]{1,0:T(8,128)S(1)} %get-tuple-element.36, f32[512,64]{1,0:T(8,128)S(1)} %get-tuple-element.34, ...), kind=kOutput, calls=%fused_computation.46 | convolution fusion | flops 3225944064 | bytes 11538944 | tf_op jit(solution)/shard_map/dot_general | solution.py:12
  112.9 2.2 collective-permute-done
  118.7 6.8 %collective-permute-done.1 = f32[128,512]{1,0:T(8,128)S(1)} collective-permute-done((f32[128,512]{1,0:T(8,128)S(1)}, f32[128,512]{1,0:T(8,128)S(1)}, u32[]{:S(2)}, u32[]{:S(2)}) %collective-permute-start.1) | collective-permute-done | bytes 262176 | tf_op jit(solution)/shard_map/ppermute | solution.py:44
  128.1 3.5 %collective-permute-done.2 = f32[64,512]{1,0:T(8,128)S(1)} collective-permute-done((f32[64,512]{1,0:T(8,128)S(1)}, f32[64,512]{1,0:T(8,128)S(1)}, u32[]{:S(2)}, u32[]{:S(2)}) %collective-permute-start.2) | collective-permute-done | bytes 131104 | tf_op jit(solution)/shard_map/ppermute | solution.py:44
  133.2 3.5 %collective-permute-done.3 = f32[64,512]{1,0:T(8,128)S(1)} collective-permute-done((f32[64,512]{1,0:T(8,128)S(1)}, f32[64,512]{1,0:T(8,128)S(1)}, u32[]{:S(2)}, u32[]{:S(2)}) %collective-permute-start.3) | collective-permute-done | bytes 131104 | tf_op jit(solution)/shard_map/ppermute | solution.py:47
  138.3 4.9 %collective-permute-done.4 = f32[128,512]{1,0:T(8,128)S(1)} collective-permute-done((f32[128,512]{1,0:T(8,128)S(1)}, f32[128,512]{1,0:T(8,128)S(1)}, u32[]{:S(2)}, u32[]{:S(2)}) %collective-permute-start.4) | collective-permute-done | bytes 262176 | tf_op jit(solution)/shard_map/ppermute | solution.py:47
  147.0 9.8 %fusion.4 = f32[512,2048]{1,0:T(8,128)S(1)} fusion(f32[2,2048,512]{2,1,0:T(8,128)} %param.7, f32[512,64]{1,0:T(8,128)S(1)} %get-tuple-element.29, f32[512,448]{1,0:T(8,128)S(1)} %get-tuple-element.31, f32[512,448]{1,0:T(8,128)S(1)} %get-tuple-element.30, f32[512,64]{1,0:T(8,128)S(1)} %get-tuple-element.28, s32[512]{0:T(512)S(1)} %iota_shift-right-logical_fusion, ...), kind=kOutput, calls=%fused_computation.10 | convolution fusion | flops 3225681920 | bytes 10490368 | tf_op jit(solution)/shard_map/dot_general | solution.py:22
  156.8 8.9 %subtract_bitcast_fusion.1 = f32[2048,512]{0,1:T(8,128)} fusion(f32[512,2048]{1,0:T(8,128)S(1)} %fusion.4, f32[512,512]{1,0:T(8,128)S(1)} %maximum_multiply_fusion, f32[2,2048,512]{2,1,0:T(8,128)S(1)} %bitcast.75), kind=kOutput, calls=%fused_computation.23 | convolution fusion | flops 3222274048 | bytes 13631488 | tf_op jit(solution)/shard_map/dot_general | solution.py:22
  165.7 12.1 %all-gather.3.cloned.1.call-done = f32[2048,512]{0,1:T(8,128)} async-done(((f32[2048,128]{0,1:T(8,128)}), f32[2048,512]{0,1:T(8,128)}) %all-gather.3.cloned.1.call-update) | async-done | bytes 4194320 | tf_op jit(solution)/shard_map/all_gather | solution.py:69
  177.8 6.5 %fusion.41 = f32[512,512]{1,0:T(8,128)S(1)} fusion(f32[2048,512]{0,1:T(8,128)} %all-gather.3.cloned.1.call-done, f32[2,2048,512]{2,1,0:T(8,128)} %param.7), kind=kOutput, calls=%fused_computation.44 | convolution fusion | flops 3221225472 | bytes 9437184 | tf_op jit(solution)/shard_map/dot_general | solution.py:12
  184.9 2.0 copy-done.2
  186.9 6.0 %fusion.44 = f32[512,512]{1,0:T(8,128)S(1)} fusion(f32[2048,512]{0,1:T(8,128)S(1)} %copy-done.2, f32[2,2048,512]{2,1,0:T(8,128)} %param.7, f32[512,64]{1,0:T(8,128)S(1)} %get-tuple-element.25, f32[512,448]{1,0:T(8,128)S(1)} %get-tuple-element.27, f32[512,448]{1,0:T(8,128)S(1)} %get-tuple-element.26, f32[512,64]{1,0:T(8,128)S(1)} %get-tuple-element.24, ...), kind=kOutput, calls=%fused_computation.45 | convolution fusion | flops 3225944064 | bytes 11538944 | tf_op jit(solution)/shard_map/dot_general | solution.py:12
  196.8 6.7 %collective-permute-done.7 = f32[128,512]{1,0:T(8,128)S(1)} collective-permute-done((f32[128,512]{1,0:T(8,128)S(1)}, f32[128,512]{1,0:T(8,128)S(1)}, u32[]{:S(2)}, u32[]{:S(2)}) %collective-permute-start.7) | collective-permute-done | bytes 262176 | tf_op jit(solution)/shard_map/ppermute | solution.py:44
  205.3 3.3 collective-permute-done.8
  210.4 3.3 collective-permute-done.9
  215.4 4.7 %collective-permute-done.10 = f32[128,512]{1,0:T(8,128)S(1)} collective-permute-done((f32[128,512]{1,0:T(8,128)S(1)}, f32[128,512]{1,0:T(8,128)S(1)}, u32[]{:S(2)}, u32[]{:S(2)}) %collective-permute-start.10) | collective-permute-done | bytes 262176 | tf_op jit(solution)/shard_map/ppermute | solution.py:47
  223.0 7.5 %fusion = f32[512,2048]{1,0:T(8,128)S(1)} fusion(f32[2,2048,512]{2,1,0:T(8,128)S(1)} %bitcast.77, f32[512,64]{1,0:T(8,128)S(1)} %get-tuple-element.19, f32[512,448]{1,0:T(8,128)S(1)} %get-tuple-element.21, f32[512,448]{1,0:T(8,128)S(1)} %get-tuple-element.20, f32[512,64]{1,0:T(8,128)S(1)} %get-tuple-element.18, s32[512]{0:T(512)S(1)} %iota_shift-right-logical_fusion, ...), kind=kOutput, calls=%fused_computation.6 | convolution fusion | flops 3225681920 | bytes 11014656 | tf_op jit(solution)/shard_map/dot_general | solution.py:22
  230.5 8.6 %subtract_bitcast_fusion = f32[2048,512]{0,1:T(8,128)} fusion(f32[512,2048]{1,0:T(8,128)S(1)} %fusion, f32[512,512]{1,0:T(8,128)S(1)} %maximum_multiply_fusion.1, f32[2,2048,512]{2,1,0:T(8,128)S(1)} %bitcast.77), kind=kOutput, calls=%fused_computation.22 | convolution fusion | flops 3222274048 | bytes 13631488 | tf_op jit(solution)/shard_map/dot_general | solution.py:22
  240.3 15.1 %reduce-scatter.3.cloned.1.call-done = f32[2048,128]{0,1:T(8,128)} async-done(((f32[2048,512]{0,1:T(8,128)}), f32[2048,128]{0,1:T(8,128)}) %reduce-scatter.3.cloned.1.call-update) | async-done | bytes 1048592 | tf_op jit(solution)/shard_map/reduce_scatter | solution.py:77
  255.4 79.5 %reduce-scatter.5.cloned.1.call-done = f32[2048,128]{0,1:T(8,128)} async-done(((f32[2048,512]{0,1:T(8,128)}), f32[2048,128]{0,1:T(8,128)}) %reduce-scatter.5.cloned.1.call-update) | async-done | bytes 1048592 | tf_op jit(solution)/shard_map/reduce_scatter | solution.py:77
  334.9 2.0 fusion.67
  (91 shorter events, 37.0 us)
Async XLA Ops:
  6.5 137.5 %copy-start = (f32[2048]{0:T(1024)S(1)}, f32[2048]{0:T(1024)}, u32[]{:S(2)}) copy-start(f32[2048]{0:T(1024)} %param.9) | copy-start | bytes 24580
  6.5 90.4 %all-gather.5.cloned.1.call-start = ((), (), s32[]{:S(2)}) async-start(), calls=%async_computation.3 | async-start | bytes 5242880 | tf_op jit(solution)/shard_map/all_gather | solution.py:69
  13.3 164.4 %all-gather.3.cloned.1.call-start = ((), (), s32[]{:S(2)}) async-start(), calls=%async_computation.2 | async-start | bytes 5242880 | tf_op jit(solution)/shard_map/all_gather | solution.py:69
  14.4 240.9 %reduce-scatter.3.cloned.1.call-start = ((), (), s32[]{:S(2)}) async-start(), calls=%async_computation.4 | async-start | bytes 5242880 | tf_op jit(solution)/shard_map/reduce_scatter | solution.py:77
  103.5 2.6 copy-start.3
  112.0 32.0 %copy-start.5 = (s32[4]{0:T(128)S(1)}, s32[4]{0:T(128)}, u32[]{:S(2)}) copy-start(s32[4]{0:T(128)} %param.10) | copy-start | bytes 52
  112.9 2.3 collective-permute-start
  117.1 8.4 %collective-permute-start.1 = (f32[128,512]{1,0:T(8,128)S(1)}, f32[128,512]{1,0:T(8,128)S(1)}, u32[]{:S(2)}, u32[]{:S(2)}) collective-permute-start(f32[128,512]{1,0:T(8,128)S(1)} %constant_dynamic-slice_fusion.4), channel_id=1, source_target_pairs={{0,8},{4,12},{8,0},{12,4},{16,24},{20,28},{24,16},{28,20},{1,9},{5... | collective-permute-start | bytes 786440 | tf_op jit(solution)/shard_map/ppermute | solution.py:44
  126.6 5.0 %collective-permute-start.2 = (f32[64,512]{1,0:T(8,128)S(1)}, f32[64,512]{1,0:T(8,128)S(1)}, u32[]{:S(2)}, u32[]{:S(2)}) collective-permute-start(f32[64,512]{1,0:T(8,128)S(1)} %constant_dynamic-slice_fusion.3), channel_id=1, source_target_pairs={{0,16},{4,20},{8,24},{12,28},{16,0},{20,4},{24,8},{28,12},{1,17},{... | collective-permute-start | bytes 393224 | tf_op jit(solution)/shard_map/ppermute | solution.py:44
  131.6 5.0 %collective-permute-start.3 = (f32[64,512]{1,0:T(8,128)S(1)}, f32[64,512]{1,0:T(8,128)S(1)}, u32[]{:S(2)}, u32[]{:S(2)}) collective-permute-start(f32[64,512]{1,0:T(8,128)S(1)} %dynamic-slice_add_fusion.5), channel_id=1, source_target_pairs={{0,16},{4,20},{8,24},{12,28},{16,0},{20,4},{24,8},{28,12},{1,17},{... | collective-permute-start | bytes 393224 | tf_op jit(solution)/shard_map/ppermute | solution.py:47
  136.7 6.4 %collective-permute-start.4 = (f32[128,512]{1,0:T(8,128)S(1)}, f32[128,512]{1,0:T(8,128)S(1)}, u32[]{:S(2)}, u32[]{:S(2)}) collective-permute-start(f32[128,512]{1,0:T(8,128)S(1)} %pad_maximum_fusion.4), channel_id=1, source_target_pairs={{0,8},{4,12},{8,0},{12,4},{16,24},{20,28},{24,16},{28,20},{1,9},{5... | collective-permute-start | bytes 786440 | tf_op jit(solution)/shard_map/ppermute | solution.py:47
  144.1 2.1 collective-permute-start.5
  146.6 10.2 %slice-start = ((s8[8388608]{0:T(1024)(128)(4,1)}), s8[4194304]{0:T(1024)(128)(4,1)S(1)}, s32[]{:S(2)}) async-start(s8[8388608]{0:T(1024)(128)(4,1)} %bitcast.74), calls=%async_computation.6 | async-start | bytes 8388608
  147.0 9.8 %slice-start.1 = ((s8[8388608]{0:T(1024)(128)(4,1)}), s8[4194304]{0:T(1024)(128)(4,1)S(1)}, s32[]{:S(2)}) async-start(s8[8388608]{0:T(1024)(128)(4,1)} %bitcast.74), calls=%async_computation.7 | async-start | bytes 8388608
  177.8 157.1 %reduce-scatter.5.cloned.1.call-start = ((), (), s32[]{:S(2)}) async-start(), calls=%async_computation.5 | async-start | bytes 5242880 | tf_op jit(solution)/shard_map/reduce_scatter | solution.py:77
  193.0 2.0 collective-permute-start.6
  194.9 28.0 %slice-start.2 = ((s8[8388608]{0:T(1024)(128)(4,1)}), s8[4194304]{0:T(1024)(128)(4,1)S(1)}, s32[]{:S(2)}) async-start(s8[8388608]{0:T(1024)(128)(4,1)} %bitcast.76), calls=%async_computation.8 | async-start | bytes 8388608
  195.1 8.4 %collective-permute-start.7 = (f32[128,512]{1,0:T(8,128)S(1)}, f32[128,512]{1,0:T(8,128)S(1)}, u32[]{:S(2)}, u32[]{:S(2)}) collective-permute-start(f32[128,512]{1,0:T(8,128)S(1)} %constant_dynamic-slice_fusion.1), channel_id=1, source_target_pairs={{0,8},{4,12},{8,0},{12,4},{16,24},{20,28},{24,16},{28,20},{1,9},{5... | collective-permute-start | bytes 786440 | tf_op jit(solution)/shard_map/ppermute | solution.py:44
  203.6 5.0 %collective-permute-start.8 = (f32[64,512]{1,0:T(8,128)S(1)}, f32[64,512]{1,0:T(8,128)S(1)}, u32[]{:S(2)}, u32[]{:S(2)}) collective-permute-start(f32[64,512]{1,0:T(8,128)S(1)} %constant_dynamic-slice_fusion), channel_id=1, source_target_pairs={{0,16},{4,20},{8,24},{12,28},{16,0},{20,4},{24,8},{28,12},{1,17},{... | collective-permute-start | bytes 393224 | tf_op jit(solution)/shard_map/ppermute | solution.py:44
  208.6 5.0 %collective-permute-start.9 = (f32[64,512]{1,0:T(8,128)S(1)}, f32[64,512]{1,0:T(8,128)S(1)}, u32[]{:S(2)}, u32[]{:S(2)}) collective-permute-start(f32[64,512]{1,0:T(8,128)S(1)} %dynamic-slice_add_fusion.4), channel_id=1, source_target_pairs={{0,16},{4,20},{8,24},{12,28},{16,0},{20,4},{24,8},{28,12},{1,17},{... | collective-permute-start | bytes 393224 | tf_op jit(solution)/shard_map/ppermute | solution.py:47
  213.7 6.4 %collective-permute-start.10 = (f32[128,512]{1,0:T(8,128)S(1)}, f32[128,512]{1,0:T(8,128)S(1)}, u32[]{:S(2)}, u32[]{:S(2)}) collective-permute-start(f32[128,512]{1,0:T(8,128)S(1)} %pad_maximum_fusion.5), channel_id=1, source_target_pairs={{0,8},{4,12},{8,0},{12,4},{16,24},{20,28},{24,16},{28,20},{1,9},{5... | collective-permute-start | bytes 786440 | tf_op jit(solution)/shard_map/ppermute | solution.py:47
  220.2 2.8 slice-start.3
  220.2 2.0 collective-permute-start.11
  337.1 3.1 copy-start.1
  (2 other events, 3.4 us)
Sparse Core Ops, SparseCore 0:
  13.4 83.4 all-gather.4
  98.5 79.2 all-gather.2
  180.1 75.2 reduce-scatter.2
  257.5 77.2 reduce-scatter.4
